TPU v7x, 512 devices: a whole 4x4x16 slice. The times are simulated.
512 devices in a mesh: orb: 512 (over z, y, x, core).
Axes of the slice: x: 4, y: 4, z: 16, core: 2. Of those that a mesh axis runs over, the one named last changes fastest.
Arguments:
- orbitals: bfloat16 [512, 48, 2304], P('orb'), may hold values from -6 to 6
- pair_mask: int32 [2, 512], replicated, may hold values from 0 to 1, as said below
- offsets: int32 [3, 2, 512], replicated, may hold values from -12 to 12
Outputs:
- exchange: bfloat16 [512, 48, 2304], P('orb')
Inputs may be any that keep to these rules, and one draw needn't show every extreme that they name: `pair_mask`: in every matching, the pair that holds orbital 0 and the pair that holds orbital 512 - 1 are live.
All inputs are finite; a program needn't handle non-finite values.
Results may differ from a plain program's by a relative error of at most 0.004.
Values may be sent and summed in bfloat16 or wider, within the bound.
No kernel may reach another device: no remote copies, remote signals or barrier semaphores. Data moves between devices by JAX's collectives and lax.ppermute only.
A program may use at most 64 MiB of HBM per device.

v0:
```python
import math

import jax
import jax.numpy as jnp
from jax import lax
from jax.sharding import PartitionSpec as P

screening = 0.5


def from_partner(block, axis, stride):
    count = lax.axis_size(axis)
    route = []
    for low in range(count):
        high = low | 1 << stride
        if high != low and high < count:
            route += [(low, high), (high, low)]
    return lax.ppermute(block, axis, route)


def sine_table(extent):
    modes = jnp.arange(1, extent + 1, dtype=jnp.int32).astype(jnp.float32)
    angles = math.pi * modes[:, None] * modes[None, :] / (extent + 1)
    return math.sqrt(2.0 / (extent + 1)) * jnp.sin(angles)


def inverse_symbol(extent):
    modes = jnp.arange(1, extent + 1, dtype=jnp.int32).astype(jnp.float32)
    eigenvalue = 2.0 - 2.0 * jnp.cos(math.pi * modes / (extent + 1))
    summed_eigen = eigenvalue[:, None, None] + eigenvalue[None, :, None] + eigenvalue[None, None, :]
    return 1.0 / (summed_eigen + screening)


def transform(volume, sines):
    extent = sines.shape[0]
    exact = lax.Precision.HIGHEST
    for turn in range(3):
        flat = jnp.dot(
            sines,
            volume.reshape(extent, extent * extent),
            precision=exact,
            preferred_element_type=jnp.float32,
        )
        volume = jnp.transpose(flat.reshape(extent, extent, extent), (1, 2, 0))
    return volume


def shift_box(volume, offset):
    extent = volume.shape[0]
    places = jnp.arange(extent, dtype=jnp.int32)
    for axis_pos in range(3):
        flat = jnp.roll(volume.reshape(extent, extent * extent), offset[axis_pos], axis=0)
        source = places - offset[axis_pos]
        inside = (source >= 0) & (source < extent)
        flat = jnp.where(inside[:, None], flat, jnp.zeros_like(flat))
        volume = jnp.transpose(flat.reshape(extent, extent, extent), (1, 2, 0))
    return volume


def pair_terms(phi_low, phi_up, offset, sines, symbol):
    visitor = shift_box(phi_up, offset)
    density = phi_low * visitor
    potential = transform(symbol * transform(density, sines), sines)
    lower_term = (potential * visitor).astype(jnp.bfloat16)
    upper_term = shift_box(potential * phi_low, -offset).astype(jnp.bfloat16)
    return (lower_term, upper_term)


def per_device(orbitals, pair_mask, offsets):
    extent = orbitals.shape[1]
    resident = orbitals.reshape(extent, extent, extent)
    sines = sine_table(extent)
    symbol = inverse_symbol(extent)
    devices = lax.axis_size("orb")
    levels = devices.bit_length() - 1
    myself = lax.axis_index("orb")
    matches = pair_mask.shape[0]
    everyone = jnp.arange(devices, dtype=jnp.int32)
    summed = jnp.zeros((extent, extent, extent), jnp.float32)

    def run_pair(operands):
        return pair_terms(*operands)

    def skip_pair(operands):
        nothing = jnp.zeros((extent, extent, extent), jnp.bfloat16)
        return (nothing, nothing)

    for match_index in range(matches):
        bit_pos = match_index * (levels - 1) // (matches - 1)
        stride = 1 << bit_pos
        is_low = myself // stride % 2 == 0
        lower_index = jnp.where(is_low, myself, myself - stride)
        chosen = everyone == lower_index
        live = jnp.sum(jnp.where(chosen, pair_mask[match_index], 0)) > 0
        offset = jnp.sum(jnp.where(chosen[None, :], offsets[:, match_index, :], 0), axis=1)
        partner_orb = from_partner(resident, "orb", bit_pos)
        phi_low = jnp.where(is_low, resident, partner_orb).astype(jnp.float32)
        phi_up = jnp.where(is_low, partner_orb, resident).astype(jnp.float32)
        lower_term, upper_term = lax.cond(
            live, run_pair, skip_pair, (phi_low, phi_up, offset, sines, symbol)
        )
        keeping = jnp.where(is_low, lower_term, upper_term)
        summed = summed + keeping.astype(jnp.float32)
    return (-summed).astype(jnp.bfloat16).reshape(1, extent, extent * extent)


def solution(mesh):
    placed = (P("orb", None, None), P(), P())
    return jax.shard_map(
        per_device, mesh=mesh, in_specs=placed, out_specs=P("orb", None, None), check_vma=False
    )
```

profile of v0, /device:TPU:51, one launch (start us, length us, event | category | flops | bytes accessed | tf_op | source)
XLA Modules:
  0.0 249.0 jit_solution(10231755837177010347)
XLA Ops:
  0.0 1.8 reshape.305
  1.8 2.6 %collective-permute-start = (bf16[48,48,48]{2,1,0:T(8,128)(2,1)S(1)}, bf16[48,48,48]{2,1,0:T(8,128)(2,1)S(1)}, u32[]{:S(2)}, u32[]{:S(2)}) collective-permute-start(bf16[48,48,48]{2,1,0:T(8,128)(2,1)S(1)} %reshape.305), channel_id=1, source_target_pairs={{0,1},{1,0},{2,3},{3,2},{4,5},{5,4},{6,7},{7,6},{8,9},{9,8},{10,11... | collective-permute-start | bytes 663560 | tf_op jit(solution)/shard_map/ppermute | solution.py:18
  4.4 14.5 %collective-permute-start.1 = (bf16[48,48,48]{2,1,0:T(8,128)(2,1)S(1)}, bf16[48,48,48]{2,1,0:T(8,128)(2,1)}, u32[]{:S(2)}, u32[]{:S(2)}) collective-permute-start(bf16[48,48,48]{2,1,0:T(8,128)(2,1)S(1)} %reshape.305), channel_id=1, source_target_pairs={{0,256},{256,0},{1,257},{257,1},{2,258},{258,2},{3,259},{259,3},{4... | collective-permute-start | bytes 663560 | tf_op jit(solution)/shard_map/ppermute | solution.py:18
  23.7 47.0 %collective-permute-done.1 = bf16[48,48,48]{2,1,0:T(8,128)(2,1)} collective-permute-done((bf16[48,48,48]{2,1,0:T(8,128)(2,1)S(1)}, bf16[48,48,48]{2,1,0:T(8,128)(2,1)}, u32[]{:S(2)}, u32[]{:S(2)}) %collective-permute-start.1) | collective-permute-done | bytes 221216 | tf_op jit(solution)/shard_map/ppermute | solution.py:18
  70.8 3.1 %select_convert_fusion.2 = (f32[48,48,48]{2,1,0:T(8,128)}, f32[48,48,48]{2,1,0:T(8,128)S(1)}, f32[48,48,48]{2,1,0:T(8,128)}, f32[48,48,48]{2,1,0:T(8,128)S(1)}) fusion(bf16[48,48,48]{2,1,0:T(8,128)(2,1)} %copy-done.1, bf16[48,48,48]{2,1,0:T(8,128)(2,1)} %copy-done.2, pred[]{:T(512)S(6)} %eq.35, bf16[48,48,48]{2,1,0:T(8,128)(2,1)} %collective-permute-done.1, ...), kind=kLoop, calls=%fused_computation.88 | loop fusion | flops 884736 | bytes 2433026 | tf_op jit(solution)/shard_map/convert_element_type | solution.py:97
  73.9 100.2 %conditional.2 = (bf16[48,48,48]{2,1,0:T(8,128)(2,1)}, bf16[48,48,48]{2,1,0:T(8,128)(2,1)}) conditional(s32[]{:T(128)} %convert_element_type.101, () %tuple.22, (s32[]{:T(128)}, s32[1,512]{1,0:T(1,128)S(1)}, s32[3,2,512]{2,1,0:T(2,128)S(1)}, s32[3,512]{1,0:T(4,128)S(1)}, f32[48,48,48]{2,1,0:T(8,128)S(1)}, /*index=5*/f32[48,48,48]{2,1,0:T(8,128)}, ...), branch_computations={%region_1.2_spmd, %region_2.5_spmd} | conditional | flops 385086112 | bytes 33716540 | solution.py:99
  78.7 1.9 fusion.12
  80.7 1.4 copy.45
  85.2 2.0 fusion.10
  87.3 1.4 copy.46
  90.6 2.0 fusion.8
  93.9 2.4 mul.24
  96.4 2.5 reshape.263
  98.9 2.3 convolution_bitcast_fusion.5
  101.2 2.4 copy.48
  103.6 2.5 reshape.265
  106.0 2.3 convolution_bitcast_fusion.4
  108.3 2.4 copy.49
  110.7 2.5 reshape.267
  113.2 2.3 convolution_bitcast_fusion.3
  115.5 2.4 copy.50
  117.9 2.4 mul.25
  120.4 2.5 %reshape.269 = f32[48,2304]{1,0:T(8,128)} reshape(f32[48,48,48]{2,1,0:T(8,128)} %mul.25) | data formatting | bytes 884736 | tf_op jit(solution)/shard_map/cond/branch_1_fun/reshape | solution.py:40
  122.9 2.3 convolution_bitcast_fusion.2
  125.1 2.4 copy.51
  127.6 2.5 reshape.271
  130.0 2.3 convolution_bitcast_fusion.1
  132.3 2.4 copy.52
  134.7 2.5 reshape.273
  137.2 2.3 convolution_bitcast_fusion
  139.5 2.4 copy.53
  141.9 2.6 %mul.45 = bf16[48,48,48]{2,1,0:T(8,128)(2,1)} multiply(f32[48,48,48]{2,1,0:T(8,128)} %bitcast.142, f32[48,48,48]{2,1,0:T(8,128)} %get-tuple-element.67) | non-fusion elementwise | flops 110592 | bytes 1105920 | tf_op jit(solution)/shard_map/cond/branch_1_fun/mul | solution.py:65
  144.5 2.3 reshape.275
  148.8 1.9 fusion.6
  150.6 2.6 %reshape.276 = bf16[48,48,48]{2,1,0:T(8,128)(2,1)} reshape(bf16[48,2304]{1,0:T(8,128)(2,1)} %fusion.6) | data formatting | bytes 442368 | tf_op jit(solution)/shard_map/cond/branch_1_fun/reshape | solution.py:56
  153.2 2.4 copy.29
  155.6 2.3 reshape.277
  158.6 1.8 fusion.4
  160.3 2.0 copy.54
  162.3 2.3 reshape.279
  165.2 1.8 fusion.2
  167.0 2.6 %convert_element_type.72 = bf16[48,48,48]{2,1,0:T(8,128)(2,1)} reshape(bf16[48,2304]{1,0:T(8,128)(2,1)} %fusion.2) | data formatting | bytes 442368 | tf_op jit(solution)/shard_map/cond/branch_1_fun/convert_element_type | solution.py:65
  169.5 2.4 copy.66
  171.9 2.2 multiply_convert_fusion
  174.1 72.0 %conditional.3 = (bf16[48,48,48]{2,1,0:T(8,128)(2,1)}, bf16[48,48,48]{2,1,0:T(8,128)(2,1)}) conditional(s32[]{:T(128)} %convert_element_type.106, () %tuple.24, (s32[]{:T(128)}, s32[1,512]{1,0:T(1,128)S(1)}, s32[3,2,512]{2,1,0:T(2,128)}, s32[3,512]{1,0:T(4,128)S(1)}, f32[48,48,48]{2,1,0:T(8,128)}, /*index=5*/f32[48,48,48]{2,1,0:T(8,128)S(1)}, ...), branch_computations={%region_5.7_spmd, %region_6.9_spmd} | conditional | flops 385086112 | bytes 33753432 | solution.py:99
  178.2 1.7 reshape.280
  180.8 1.4 copy.55
  185.5 2.0 fusion.25
  190.7 2.0 fusion.23
  195.3 2.5 %reshape.286 = f32[48,2304]{1,0:T(8,128)} reshape(f32[48,48,48]{2,1,0:T(8,128)} %mul.46) | data formatting | bytes 884736 | tf_op jit(solution)/shard_map/cond/branch_1_fun/reshape | solution.py:40
  197.8 2.3 convolution_bitcast_fusion.11
  200.1 2.4 copy.58
  202.5 2.5 %reshape.288 = f32[48,2304]{1,0:T(8,128)} reshape(f32[48,48,48]{2,1,0:T(8,128)} %bitcast.156) | data formatting | bytes 884736 | tf_op jit(solution)/shard_map/cond/branch_1_fun/reshape | solution.py:40
  205.0 2.3 convolution_bitcast_fusion.10
  207.3 2.4 copy.59
  209.7 2.5 %reshape.290 = f32[48,2304]{1,0:T(8,128)} reshape(f32[48,48,48]{2,1,0:T(8,128)} %bitcast.157) | data formatting | bytes 884736 | tf_op jit(solution)/shard_map/cond/branch_1_fun/reshape | solution.py:40
  212.2 2.3 convolution_bitcast_fusion.9
  214.5 2.4 copy.60
  216.9 2.4 mul.47
  219.3 1.7 reshape.292
  225.0 2.3 convolution_bitcast_fusion.7
  229.9 2.3 convolution_bitcast_fusion.6
  234.6 1.6 reshape.298
  246.1 1.6 negate_convert_fusion
  (70 shorter events, 44.0 us)
Async XLA Ops:
  0.0 19.5 %copy-start.4 = (s32[2,512]{1,0:T(2,128)S(1)}, s32[2,512]{1,0:T(2,128)}, u32[]{:S(2)}) copy-start(s32[2,512]{1,0:T(2,128)} %param.10) | copy-start | bytes 12292
  1.8 21.1 %copy-start.1 = (bf16[48,48,48]{2,1,0:T(8,128)(2,1)}, bf16[48,48,48]{2,1,0:T(8,128)(2,1)S(1)}, u32[]{:S(2)}) copy-start(bf16[48,48,48]{2,1,0:T(8,128)(2,1)S(1)} %reshape.305) | copy-start | bytes 663556
  1.8 21.1 %collective-permute-start = (bf16[48,48,48]{2,1,0:T(8,128)(2,1)S(1)}, bf16[48,48,48]{2,1,0:T(8,128)(2,1)S(1)}, u32[]{:S(2)}, u32[]{:S(2)}) collective-permute-start(bf16[48,48,48]{2,1,0:T(8,128)(2,1)S(1)} %reshape.305), channel_id=1, source_target_pairs={{0,1},{1,0},{2,3},{3,2},{4,5},{5,4},{6,7},{7,6},{8,9},{9,8},{10,11... | collective-permute-start | bytes 663560 | tf_op jit(solution)/shard_map/ppermute | solution.py:18
  4.4 66.4 %collective-permute-start.1 = (bf16[48,48,48]{2,1,0:T(8,128)(2,1)S(1)}, bf16[48,48,48]{2,1,0:T(8,128)(2,1)}, u32[]{:S(2)}, u32[]{:S(2)}) collective-permute-start(bf16[48,48,48]{2,1,0:T(8,128)(2,1)S(1)} %reshape.305), channel_id=1, source_target_pairs={{0,256},{256,0},{1,257},{257,1},{2,258},{258,2},{3,259},{259,3},{4... | collective-permute-start | bytes 663560 | tf_op jit(solution)/shard_map/ppermute | solution.py:18
  22.9 51.0 %copy-start.3 = (s32[3,2,512]{2,1,0:T(2,128)S(1)}, s32[3,2,512]{2,1,0:T(2,128)}, u32[]{:S(2)}) copy-start(s32[3,2,512]{2,1,0:T(2,128)} %param.11) | copy-start | bytes 36868
  22.9 0.8 copy-start.2
  219.3 1.7 copy-start
where the time goes:
time: 252 us; the launch traced here: 249 us
  local copies, waits for them, and re-layouts  101 us (40%)
  other arithmetic  47.2 us (19%)
  waiting for transfers between devices  47 us (19%)
  matrix products  26.5 us (11%)
  starting transfers between devices  17.1 us (7%)
  loops' own time  8.23 us (3%)
    ppermute x2, waiting for transfers between devices, from_partner(): return lax.ppermute(block, axis, route)  47 us
    reshape x12, local copies, waits for them, and re-layouts, transform(): volume.reshape(extent, extent * extent)  26.6 us
    dot_general x12, matrix products, transform(): jnp.dot(sines, volume.reshape(extent, extent * extent), precision=exact,...  26.5 us
    reshape x12, local copies, waits for them, and re-layouts, transform(): volume = jnp.transpose(flat.reshape(extent, extent, extent), (1, 2, 0))  25.8 us
    reshape x12, local copies, waits for them, and re-layouts, shift_box(): volume.reshape(extent, extent * extent)  17.6 us
    ppermute x2, starting transfers between devices, from_partner(): return lax.ppermute(block, axis, route)  17.1 us
    select_n x10, other arithmetic, shift_box(): flat = jnp.where(inside[:, None], flat, jnp.zeros_like(flat))  14.9 us
    reshape x10, local copies, waits for them, and re-layouts, shift_box(): volume = jnp.transpose(flat.reshape(extent, extent, extent), (1, 2, 0))  14 us
  transfers between devices with their start and end apart: 2, of which 1 were waited for; matrix products, arithmetic and copies ran while one was open for 1% of the time, Pallas kernels for 0%

commit v1 on v0

v1 whole, which is shorter than its diff:
```python
import jax
import jax.numpy as jnp
import numpy as np
from jax import lax
from jax.experimental import pallas as pl
from jax.experimental.pallas import tpu as pltpu
from jax.sharding import PartitionSpec as P

SCREENING = 0.5
BOX = 48
WIDE = 64
LANES = 128
FLAT = BOX * BOX
TILES = FLAT // LANES
GROUPS = 6
PAIRS = BOX // 2
EDGE = 5
ROWPAD = 16
ROWS = BOX + 2 * ROWPAD

F32 = jnp.float32
BF16 = jnp.bfloat16


def split_np(table):
    high = table.astype(np.float32).astype(jnp.bfloat16)
    low = (table - high.astype(np.float64)).astype(np.float32).astype(jnp.bfloat16)
    return high, low


def tables():
    modes = np.arange(1, BOX + 1, dtype=np.float64)
    sines = np.sqrt(2.0 / (BOX + 1)) * np.sin(np.pi * modes[:, None] * modes[None, :] / (BOX + 1))
    eigen = 2.0 - 2.0 * np.cos(np.pi * modes / (BOX + 1))

    def stacked(matrix):
        high, low = split_np(matrix)
        return np.concatenate([high, high, low], axis=1)

    order = np.concatenate([np.arange(0, BOX, 2), np.arange(1, BOX, 2)])
    over_a = stacked(sines)
    over_b = stacked(sines[:, order])
    back_b = stacked(sines[order, :])
    narrow = np.zeros((8 * BOX, 8 * WIDE))
    for row in range(8):
        narrow[row * BOX : (row + 1) * BOX, row * WIDE : row * WIDE + BOX] = sines
    fore_c = np.stack([narrow[0:256, 0:256], narrow[128:384, 256:512]])
    widened = narrow.T
    back_c = np.stack([widened[128 * n : 128 * n + 256, 128 * n : 128 * n + 128] for n in range(3)])
    symbol = np.zeros((BOX, BOX, WIDE))
    symbol[:, :, :BOX] = 1.0 / (
        eigen[:, None, None] + eigen[None, :, None] + eigen[None, None, :] + SCREENING
    )
    symbol = np.transpose(symbol, (1, 0, 2)).reshape(BOX, BOX * WIDE).astype(np.float32)
    fore_c = np.stack(split_np(fore_c))
    back_c = np.stack(split_np(back_c))
    return over_a, over_b, back_b, fore_c, back_c, symbol


def split(x):
    high = x.astype(BF16)
    low = (x - high.astype(F32)).astype(BF16)
    return high, low


def apply_rows(matrix, x):
    high, low = split(x)
    return jnp.dot(matrix, jnp.concatenate([high, low, high], axis=0), preferred_element_type=F32)


def apply_lanes(parts, table):
    splits = [split(x) for x in parts]
    highs = jnp.concatenate([h for h, _ in splits], axis=0)
    lows = jnp.concatenate([l for _, l in splits], axis=0)
    out = jnp.dot(highs, table[0], preferred_element_type=F32)
    out = out + jnp.dot(lows, table[0], preferred_element_type=F32)
    out = out + jnp.dot(highs, table[1], preferred_element_type=F32)
    return [out[BOX * i : BOX * (i + 1)] for i in range(len(parts))]


def make_kernel(match_index, bit_pos, last):
    def kernel(*refs):
        me_ref, mask_ref, off_ref, mine_ref, partner_ref = refs[:5]
        at = 5
        if last:
            prev_ref = refs[at]
            at += 1
        over_a_ref, over_b_ref, back_b_ref, fore_c_ref, back_c_ref, symbol_ref = refs[at : at + 6]
        out_ref, pad_ref, flip_ref = refs[at + 6 :]

        me = me_ref[0]
        upper_bit = (me >> bit_pos) & 1
        lower = me - (upper_bit << bit_pos)
        is_low = upper_bit == 0
        live = mask_ref[match_index, lower] > 0
        off = [off_ref[d, match_index, lower] for d in range(3)]

        lane = lax.broadcasted_iota(jnp.int32, (1, LANES), 1)

        def fill(tiles):
            for j in range(TILES):
                pad_ref[EDGE + j, ROWPAD : ROWPAD + BOX, :] = tiles[j]

        def shifted(o):
            start = EDGE * LANES - (o[1] * BOX + o[2])
            tile = start >> 7
            rest = start & (LANES - 1)
            turn = (LANES - rest) & (LANES - 1)
            keep = lane < LANES - rest
            rows = pl.ds(ROWPAD - o[0], BOX)
            rolled = [pltpu.roll(pad_ref[tile + j, rows, :], turn, axis=1) for j in range(TILES + 1)]
            result = []
            for j in range(TILES):
                flat = lane + LANES * j
                place = flat - ((flat * 43691) >> 21) * BOX - o[2]
                inside = jnp.where((place >= 0) & (place < BOX), 1.0, 0.0).astype(F32)
                here = jnp.where(keep, inside, 0.0)
                there = inside - here
                result.append(rolled[j] * here + rolled[j + 1] * there)
            return result

        def tile_of(ref, j):
            return ref[0, :, LANES * j : LANES * (j + 1)].astype(F32)

        def emit(j, term):
            cols = slice(LANES * j, LANES * (j + 1))
            if last:
                out_ref[0, :, cols] = (-(prev_ref[0, :, cols].astype(F32) + term)).astype(BF16)
            else:
                out_ref[0, :, cols] = term.astype(BF16)

        @pl.when(live)
        def _():
            zero_rows = jnp.zeros((ROWS, LANES), F32)
            for j in range(2 * EDGE + TILES):
                pad_ref[j] = zero_rows
            low_f = jnp.where(is_low, 1.0, 0.0).astype(F32)
            low_v = jnp.full((1, LANES), low_f, F32) > 0.5
            mine = [tile_of(mine_ref, j) for j in range(TILES)]
            partner = [tile_of(partner_ref, j) for j in range(TILES)]
            fill([jnp.where(low_v, p, m) for p, m in zip(partner, mine)])
            visitor = shifted(off)
            other = [jnp.where(low_v, m, p) for p, m in zip(partner, mine)]
            density = [o * v for o, v in zip(other, visitor)]
            factor = [jnp.where(low_v, v, o) for o, v in zip(other, visitor)]

            over_a = over_a_ref[...]
            wide = [
                apply_rows(over_a, jnp.concatenate(density[3 * g : 3 * g + 3], axis=1))
                for g in range(GROUPS)
            ]
            for h in range(2):
                got = apply_lanes(
                    [w[:, LANES * h : LANES * h + 256] for w in wide], (fore_c_ref[0, h], fore_c_ref[1, h])
                )
                for g in range(GROUPS):
                    for k in range(2):
                        row = (4 * g + 2 * h + k) * BOX
                        flip_ref[row : row + BOX, :] = got[g][:, LANES * k : LANES * (k + 1)]

            over_b = over_b_ref[...]
            back_b = back_b_ref[...]
            first = lane < WIDE
            backs = []
            for pair in range(PAIRS // 2):
                cols = []
                for u in (2 * pair, 2 * pair + 1):
                    even = flip_ref[pl.ds(2 * u, PAIRS, stride=BOX), :]
                    odd = flip_ref[pl.ds(2 * u + 1, PAIRS, stride=BOX), :]
                    upper = jnp.where(first, even, pltpu.roll(odd, WIDE, axis=1))
                    under = jnp.where(first, pltpu.roll(even, WIDE, axis=1), odd)
                    cols.append(jnp.concatenate([upper, under], axis=0))
                modes = apply_rows(over_b, jnp.concatenate(cols, axis=1))
                modes = modes * symbol_ref[:, 256 * pair : 256 * (pair + 1)]
                backs.append(apply_rows(back_b, modes))
            for pair in range(PAIRS // 2):
                for k in range(2):
                    u = 2 * pair + k
                    block = backs[pair][:, LANES * k : LANES * (k + 1)]
                    upper, under = block[:PAIRS], block[PAIRS:]
                    even = jnp.where(first, upper, pltpu.roll(under, WIDE, axis=1))
                    odd = jnp.where(first, pltpu.roll(upper, WIDE, axis=1), under)
                    flip_ref[pl.ds(2 * u, PAIRS, stride=BOX), :] = even
                    flip_ref[pl.ds(2 * u + 1, PAIRS, stride=BOX), :] = odd

            narrow = [[None] * 3 for _ in range(GROUPS)]
            for n in range(3):
                parts = []
                for g in range(GROUPS):
                    row = (4 * g + n) * BOX
                    parts.append(
                        jnp.concatenate(
                            [flip_ref[row : row + BOX, :], flip_ref[row + BOX : row + 2 * BOX, :]], axis=1
                        )
                    )
                got = apply_lanes(parts, (back_c_ref[0, n], back_c_ref[1, n]))
                for g in range(GROUPS):
                    narrow[g][n] = got[g]
            product = []
            for g in range(GROUPS):
                potential = apply_rows(over_a, jnp.concatenate(narrow[g], axis=1))
                for n in range(3):
                    product.append(potential[:, LANES * n : LANES * (n + 1)] * factor[3 * g + n])
            fill([p.astype(BF16).astype(F32) for p in product])
            term = shifted([jnp.where(is_low, 0, -o) for o in off])
            for j in range(TILES):
                emit(j, term[j])

        @pl.when(jnp.logical_not(live))
        def _():
            nothing = jnp.zeros((BOX, LANES), F32)
            for j in range(TILES):
                emit(j, nothing)

    return kernel


def pair_call(match_index, bit_pos, last, me, pair_mask, offsets, mine, partner, prev, consts):
    smem = pl.BlockSpec(memory_space=pltpu.SMEM)
    vmem = pl.BlockSpec(memory_space=pltpu.VMEM)
    operands = [me, pair_mask, offsets, mine, partner] + ([prev] if last else []) + list(consts)
    specs = [smem] * 3 + [vmem] * (len(operands) - 3)
    return pl.pallas_call(
        make_kernel(match_index, bit_pos, last),
        out_shape=jax.ShapeDtypeStruct(mine.shape, BF16),
        in_specs=specs,
        out_specs=vmem,
        scratch_shapes=[
            pltpu.VMEM((2 * EDGE + TILES, ROWS, LANES), F32),
            pltpu.VMEM((PAIRS * BOX, LANES), F32),
        ],
        name="pair_last" if last else "pair_first",
    )(*operands)


def from_partner(block, axis, stride):
    count = lax.axis_size(axis)
    route = []
    for low in range(count):
        high = low | 1 << stride
        if high != low and high < count:
            route += [(low, high), (high, low)]
    return lax.ppermute(block, axis, route)


def per_device(orbitals, pair_mask, offsets):
    devices = lax.axis_size("orb")
    levels = devices.bit_length() - 1
    me = lax.axis_index("orb").astype(jnp.int32).reshape(1)
    matches = pair_mask.shape[0]
    consts = [jnp.asarray(t) for t in tables()]
    bits = [m * (levels - 1) // (matches - 1) for m in range(matches)]
    partners = [from_partner(orbitals, "orb", bit) for bit in bits]
    near = pair_call(0, bits[0], False, me, pair_mask, offsets, orbitals, partners[0], None, consts)
    return pair_call(1, bits[1], True, me, pair_mask, offsets, orbitals, partners[1], near, consts)


def solution(mesh):
    placed = (P("orb", None, None), P(), P())
    return jax.shard_map(
        per_device, mesh=mesh, in_specs=placed, out_specs=P("orb", None, None), check_vma=False
    )
```

time: 252 us -> 43.3 us (0.17)
  the two profiles are of different devices: /device:TPU:51 before, /device:TPU:48 now
where the time goes in v1:
time: 43.3 us; the launch traced here: 43.1 us
  waiting for transfers between devices  17.8 us (41%)
  starting transfers between devices  16.7 us (39%)
  Pallas kernels  7.19 us (17%)
  local copies, waits for them, and re-layouts  1.36 us (3%)
    ppermute x2, waiting for transfers between devices, from_partner(): return lax.ppermute(block, axis, route)  17.8 us
    ppermute x2, starting transfers between devices, from_partner(): return lax.ppermute(block, axis, route)  16.7 us
    pallas_call x2, Pallas kernels, pair_call(): pl.pallas_call(make_kernel(match_index, bit_pos, last), out_shape=jax.Sha...  7.19 us
    unnamed x4, local copies, waits for them, and re-layouts  1.36 us
  transfers between devices with their start and end apart: 2, of which 1 were waited for; matrix products, arithmetic and copies ran while one was open for 0% of the time, Pallas kernels for 5%

profile of v1, /device:TPU:48, one launch (start us, length us, event | category | flops | bytes accessed | tf_op | source)
XLA Modules:
  0.0 43.1 jit_solution(1526694906718782375)
XLA Ops:
  0.0 1.9 %collective-permute-start.1 = (bf16[1,48,2304]{2,1,0:T(8,128)(2,1)}, bf16[1,48,2304]{2,1,0:T(8,128)(2,1)S(1)}, u32[]{:S(2)}, u32[]{:S(2)}) collective-permute-start(bf16[1,48,2304]{2,1,0:T(8,128)(2,1)} %refs_3_.3), channel_id=1, source_target_pairs={{0,1},{1,0},{2,3},{3,2},{4,5},{5,4},{6,7},{7,6},{8,9},{9,8},{10,11... | collective-permute-start | bytes 663560 | tf_op jit(solution)/shard_map/ppermute | solution.py:243
  1.9 14.8 %collective-permute-start = (bf16[1,48,2304]{2,1,0:T(8,128)(2,1)}, bf16[1,48,2304]{2,1,0:T(8,128)(2,1)S(1)}, u32[]{:S(2)}, u32[]{:S(2)}) collective-permute-start(bf16[1,48,2304]{2,1,0:T(8,128)(2,1)} %refs_3_.3), channel_id=1, source_target_pairs={{0,256},{256,0},{1,257},{257,1},{2,258},{258,2},{3,259},{259,3},{4... | collective-permute-start | bytes 663560 | tf_op jit(solution)/shard_map/ppermute | solution.py:243
  16.8 0.0 collective-permute-done.1.refs_4_
  16.8 0.0 copy-start
  16.8 0.7 %copy-done = bf16[1,48,2304]{2,1,0:T(8,128)(2,1)} copy-done((bf16[1,48,2304]{2,1,0:T(8,128)(2,1)}, bf16[1,48,2304]{2,1,0:T(8,128)(2,1)S(1)}, u32[]{:S(2)}) %copy-start) | copy-done | bytes 221208
  17.5 2.3 %pair_first.1.refs_5_ = bf16[1,48,2304]{2,1,0:T(8,128)(2,1)} custom-call(s32[1]{0:T(128)} %bitcast.refs_0_, s32[2,512]{1,0:T(2,128)} %refs_1_.3, s32[3,2,512]{2,1,0:T(2,128)} %refs_2_.3, bf16[1,48,2304]{2,1,0:T(8,128)(2,1)} %refs_3_.3, bf16[1,48,2304]{2,1,0:T(8,128)(2,1)} %copy-done, bf16[48,144]{1,0:T(8,128)(2,1)} %constant.16.clone.refs_5_.refs_6_, ...), custom_call_target="tpu_custom_call" | custom-call | tf_op jit(solution)/shard_map/pair_first/pallas_call | solution.py:223
  19.8 17.8 %collective-permute-done.refs_4_ = bf16[1,48,2304]{2,1,0:T(8,128)(2,1)S(1)} collective-permute-done((bf16[1,48,2304]{2,1,0:T(8,128)(2,1)}, bf16[1,48,2304]{2,1,0:T(8,128)(2,1)S(1)}, u32[]{:S(2)}, u32[]{:S(2)}) %collective-permute-start) | collective-permute-done | bytes 221216 | tf_op jit(solution)/shard_map/ppermute | solution.py:243
  37.5 0.0 copy-start.1
  37.5 0.7 %copy-done.1 = bf16[1,48,2304]{2,1,0:T(8,128)(2,1)} copy-done((bf16[1,48,2304]{2,1,0:T(8,128)(2,1)}, bf16[1,48,2304]{2,1,0:T(8,128)(2,1)S(1)}, u32[]{:S(2)}) %copy-start.1) | copy-done | bytes 221208
  38.2 4.9 %pair_last.1 = bf16[1,48,2304]{2,1,0:T(8,128)(2,1)} custom-call(s32[1]{0:T(128)} %bitcast.refs_0_, s32[2,512]{1,0:T(2,128)} %refs_1_.3, s32[3,2,512]{2,1,0:T(2,128)} %refs_2_.3, bf16[1,48,2304]{2,1,0:T(8,128)(2,1)} %refs_3_.3, bf16[1,48,2304]{2,1,0:T(8,128)(2,1)} %copy-done.1, bf16[1,48,2304]{2,1,0:T(8,128)(2,1)} %pair_first.1.refs_5_, ...), custom_call_target="tpu_custom_call" | custom-call | tf_op jit(solution)/shard_map/pair_last/pallas_call | solution.py:223
Async XLA Ops:
  0.0 16.8 %collective-permute-start.1 = (bf16[1,48,2304]{2,1,0:T(8,128)(2,1)}, bf16[1,48,2304]{2,1,0:T(8,128)(2,1)S(1)}, u32[]{:S(2)}, u32[]{:S(2)}) collective-permute-start(bf16[1,48,2304]{2,1,0:T(8,128)(2,1)} %refs_3_.3), channel_id=1, source_target_pairs={{0,1},{1,0},{2,3},{3,2},{4,5},{5,4},{6,7},{7,6},{8,9},{9,8},{10,11... | collective-permute-start | bytes 663560 | tf_op jit(solution)/shard_map/ppermute | solution.py:243
  1.9 35.6 %collective-permute-start = (bf16[1,48,2304]{2,1,0:T(8,128)(2,1)}, bf16[1,48,2304]{2,1,0:T(8,128)(2,1)S(1)}, u32[]{:S(2)}, u32[]{:S(2)}) collective-permute-start(bf16[1,48,2304]{2,1,0:T(8,128)(2,1)} %refs_3_.3), channel_id=1, source_target_pairs={{0,256},{256,0},{1,257},{257,1},{2,258},{258,2},{3,259},{259,3},{4... | collective-permute-start | bytes 663560 | tf_op jit(solution)/shard_map/ppermute | solution.py:243
  16.8 0.7 %copy-start = (bf16[1,48,2304]{2,1,0:T(8,128)(2,1)}, bf16[1,48,2304]{2,1,0:T(8,128)(2,1)S(1)}, u32[]{:S(2)}) copy-start(bf16[1,48,2304]{2,1,0:T(8,128)(2,1)S(1)} %collective-permute-done.1.refs_4_) | copy-start | bytes 663556
  37.5 0.7 %copy-start.1 = (bf16[1,48,2304]{2,1,0:T(8,128)(2,1)}, bf16[1,48,2304]{2,1,0:T(8,128)(2,1)S(1)}, u32[]{:S(2)}) copy-start(bf16[1,48,2304]{2,1,0:T(8,128)(2,1)S(1)} %collective-permute-done.refs_4_) | copy-start | bytes 663556

commit v2 on v1

--- a/solution.py
+++ b/solution.py
@@ -5,6 +5,7 @@
 from jax.experimental import pallas as pl
 from jax.experimental.pallas import tpu as pltpu
 from jax.sharding import PartitionSpec as P
+
 
 SCREENING = 0.5
 BOX = 48
@@ -229,6 +230,7 @@
             pltpu.VMEM((2 * EDGE + TILES, ROWS, LANES), F32),
             pltpu.VMEM((PAIRS * BOX, LANES), F32),
         ],
+        compiler_params=pltpu.CompilerParams(vmem_limit_bytes=16 * 2**20),
         name="pair_last" if last else "pair_first",
     )(*operands)
 
@@ -250,9 +252,10 @@
     matches = pair_mask.shape[0]
     consts = [jnp.asarray(t) for t in tables()]
     bits = [m * (levels - 1) // (matches - 1) for m in range(matches)]
-    partners = [from_partner(orbitals, "orb", bit) for bit in bits]
-    near = pair_call(0, bits[0], False, me, pair_mask, offsets, orbitals, partners[0], None, consts)
-    return pair_call(1, bits[1], True, me, pair_mask, offsets, orbitals, partners[1], near, consts)
+    far = from_partner(orbitals, "orb", bits[1])
+    near = from_partner(orbitals, "orb", bits[0])
+    first = pair_call(0, bits[0], False, me, pair_mask, offsets, orbitals, near, None, consts)
+    return pair_call(1, bits[1], True, me, pair_mask, offsets, orbitals, far, first, consts)
 
 
 def solution(mesh):

time: 43.3 us -> 42.3 us (0.977)
  the two profiles are of different devices: /device:TPU:48 before, /device:TPU:32 now
where the time goes in v2:
time: 42.3 us; the launch traced here: 41.7 us
  starting transfers between devices  16.9 us (40%)
  waiting for transfers between devices  10.5 us (25%)
  Pallas kernels  7.36 us (17%)
  local copies, waits for them, and re-layouts  6.96 us (16%)
    ppermute x2, starting transfers between devices, from_partner(): return lax.ppermute(block, axis, route)  16.9 us
    ppermute x2, waiting for transfers between devices, from_partner(): return lax.ppermute(block, axis, route)  10.5 us
    pallas_call x2, Pallas kernels, pair_call(): pl.pallas_call(make_kernel(match_index, bit_pos, last), out_shape=jax.Sha...  7.36 us
    unnamed x22, local copies, waits for them, and re-layouts  6.96 us
  transfers between devices with their start and end apart: 2, of which 1 were waited for; matrix products, arithmetic and copies ran while one was open for 0% of the time, Pallas kernels for 8%

profile of v2, /device:TPU:32, one launch (start us, length us, event | category | flops | bytes accessed | tf_op | source)
XLA Modules:
  0.0 41.7 jit_solution(10963666092938849199)
XLA Ops:
  0.0 0.0 copy-start.10
  0.0 2.0 %collective-permute-start.1 = (bf16[1,48,2304]{2,1,0:T(8,128)(2,1)}, bf16[1,48,2304]{2,1,0:T(8,128)(2,1)S(1)}, u32[]{:S(2)}, u32[]{:S(2)}) collective-permute-start(bf16[1,48,2304]{2,1,0:T(8,128)(2,1)} %refs_3_.3), channel_id=1, source_target_pairs={{0,1},{1,0},{2,3},{3,2},{4,5},{5,4},{6,7},{7,6},{8,9},{9,8},{10,11... | collective-permute-start | bytes 663560 | tf_op jit(solution)/shard_map/ppermute | solution.py:245
  2.0 14.8 %collective-permute-start = (bf16[1,48,2304]{2,1,0:T(8,128)(2,1)}, bf16[1,48,2304]{2,1,0:T(8,128)(2,1)S(1)}, u32[]{:S(2)}, u32[]{:S(2)}) collective-permute-start(bf16[1,48,2304]{2,1,0:T(8,128)(2,1)} %refs_3_.3), channel_id=1, source_target_pairs={{0,256},{256,0},{1,257},{257,1},{2,258},{258,2},{3,259},{259,3},{4... | collective-permute-start | bytes 663560 | tf_op jit(solution)/shard_map/ppermute | solution.py:245
  16.9 0.0 collective-permute-done.1.refs_4_
  16.9 0.0 copy-done.10
  16.9 0.0 copy-start
  16.9 1.1 %copy-done = f32[48,3072]{1,0:T(8,128)S(1)} copy-done((f32[48,3072]{1,0:T(8,128)S(1)}, f32[48,3072]{1,0:T(8,128)}, u32[]{:S(2)}) %copy-start) | copy-done | bytes 589848
  18.0 0.0 copy-start.2
  18.0 1.0 %copy-done.2 = bf16[2,2,256,256]{3,2,1,0:T(8,128)(2,1)S(1)} copy-done((bf16[2,2,256,256]{3,2,1,0:T(8,128)(2,1)S(1)}, bf16[2,2,256,256]{3,2,1,0:T(8,128)(2,1)}, u32[]{:S(2)}) %copy-start.2) | copy-done | bytes 524312
  19.0 0.0 copy-start.4
  19.0 1.0 %copy-done.4 = bf16[2,3,256,128]{3,2,1,0:T(8,128)(2,1)S(1)} copy-done((bf16[2,3,256,128]{3,2,1,0:T(8,128)(2,1)S(1)}, bf16[2,3,256,128]{3,2,1,0:T(8,128)(2,1)}, u32[]{:S(2)}) %copy-start.4) | copy-done | bytes 393240
  20.0 0.0 copy-start.5
  20.0 0.9 %copy-done.5 = bf16[1,48,2304]{2,1,0:T(8,128)(2,1)S(1)} copy-done((bf16[1,48,2304]{2,1,0:T(8,128)(2,1)S(1)}, bf16[1,48,2304]{2,1,0:T(8,128)(2,1)}, u32[]{:S(2)}) %copy-start.5) | copy-done | bytes 221208
  20.9 0.0 copy-start.6
  21.0 0.7 %copy-done.6 = bf16[48,144]{1,0:T(8,128)(2,1)S(1)} copy-done((bf16[48,144]{1,0:T(8,128)(2,1)S(1)}, bf16[48,144]{1,0:T(8,128)(2,1)}, u32[]{:S(2)}) %copy-start.6) | copy-done | bytes 13848
  21.7 0.0 copy-start.7
  21.7 0.7 %copy-done.7 = bf16[48,144]{1,0:T(8,128)(2,1)S(1)} copy-done((bf16[48,144]{1,0:T(8,128)(2,1)S(1)}, bf16[48,144]{1,0:T(8,128)(2,1)}, u32[]{:S(2)}) %copy-start.7) | copy-done | bytes 13848
  22.4 0.0 copy-start.8
  22.4 0.7 %copy-done.8 = bf16[48,144]{1,0:T(8,128)(2,1)S(1)} copy-done((bf16[48,144]{1,0:T(8,128)(2,1)S(1)}, bf16[48,144]{1,0:T(8,128)(2,1)}, u32[]{:S(2)}) %copy-start.8) | copy-done | bytes 13848
  23.2 0.0 copy-start.9
  23.2 0.7 %copy-done.9 = s32[3,2,512]{2,1,0:T(2,128)S(1)} copy-done((s32[3,2,512]{2,1,0:T(2,128)S(1)}, s32[3,2,512]{2,1,0:T(2,128)}, u32[]{:S(2)}) %copy-start.9) | copy-done | bytes 12312
  23.9 0.0 copy-start.1
  23.9 0.0 copy-start.3
  23.9 3.3 %pair_first.1.refs_5_ = bf16[1,48,2304]{2,1,0:T(8,128)(2,1)S(1)} custom-call(s32[1]{0:T(128)} %bitcast.refs_0_, s32[2,512]{1,0:T(2,128)S(1)} %copy-done.10, s32[3,2,512]{2,1,0:T(2,128)S(1)} %copy-done.9, bf16[1,48,2304]{2,1,0:T(8,128)(2,1)S(1)} %copy-done.5, bf16[1,48,2304]{2,1,0:T(8,128)(2,1)S(1)} %collective-permute-done.1.refs_4_, ...), custom_call_target="tpu_custom_call" | custom-call | tf_op jit(solution)/shard_map/pair_first/pallas_call | solution.py:224
  27.2 10.5 %collective-permute-done.refs_4_ = bf16[1,48,2304]{2,1,0:T(8,128)(2,1)S(1)} collective-permute-done((bf16[1,48,2304]{2,1,0:T(8,128)(2,1)}, bf16[1,48,2304]{2,1,0:T(8,128)(2,1)S(1)}, u32[]{:S(2)}, u32[]{:S(2)}) %collective-permute-start) | collective-permute-done | bytes 221216 | tf_op jit(solution)/shard_map/ppermute | solution.py:245
  37.7 0.0 copy-done.1
  37.7 0.0 copy-done.3
  37.7 4.0 %pair_last.1 = bf16[1,48,2304]{2,1,0:T(8,128)(2,1)} custom-call(s32[1]{0:T(128)} %bitcast.refs_0_, s32[2,512]{1,0:T(2,128)S(1)} %copy-done.10, s32[3,2,512]{2,1,0:T(2,128)S(1)} %copy-done.9, bf16[1,48,2304]{2,1,0:T(8,128)(2,1)S(1)} %copy-done.5, bf16[1,48,2304]{2,1,0:T(8,128)(2,1)S(1)} %collective-permute-done.refs_4_, ...), custom_call_target="tpu_custom_call" | custom-call | tf_op jit(solution)/shard_map/pair_last/pallas_call | solution.py:224
Async XLA Ops:
  0.0 16.9 %copy-start.10 = (s32[2,512]{1,0:T(2,128)S(1)}, s32[2,512]{1,0:T(2,128)}, u32[]{:S(2)}) copy-start(s32[2,512]{1,0:T(2,128)} %refs_1_.3) | copy-start | bytes 12292
  0.0 16.9 %collective-permute-start.1 = (bf16[1,48,2304]{2,1,0:T(8,128)(2,1)}, bf16[1,48,2304]{2,1,0:T(8,128)(2,1)S(1)}, u32[]{:S(2)}, u32[]{:S(2)}) collective-permute-start(bf16[1,48,2304]{2,1,0:T(8,128)(2,1)} %refs_3_.3), channel_id=1, source_target_pairs={{0,1},{1,0},{2,3},{3,2},{4,5},{5,4},{6,7},{7,6},{8,9},{9,8},{10,11... | collective-permute-start | bytes 663560 | tf_op jit(solution)/shard_map/ppermute | solution.py:245
  2.0 35.6 %collective-permute-start = (bf16[1,48,2304]{2,1,0:T(8,128)(2,1)}, bf16[1,48,2304]{2,1,0:T(8,128)(2,1)S(1)}, u32[]{:S(2)}, u32[]{:S(2)}) collective-permute-start(bf16[1,48,2304]{2,1,0:T(8,128)(2,1)} %refs_3_.3), channel_id=1, source_target_pairs={{0,256},{256,0},{1,257},{257,1},{2,258},{258,2},{3,259},{259,3},{4... | collective-permute-start | bytes 663560 | tf_op jit(solution)/shard_map/ppermute | solution.py:245
  16.9 1.1 %copy-start = (f32[48,3072]{1,0:T(8,128)S(1)}, f32[48,3072]{1,0:T(8,128)}, u32[]{:S(2)}) copy-start(f32[48,3072]{1,0:T(8,128)} %constant.21.clone.refs_10_.refs_11_) | copy-start | bytes 1769476
  18.0 1.0 %copy-start.2 = (bf16[2,2,256,256]{3,2,1,0:T(8,128)(2,1)S(1)}, bf16[2,2,256,256]{3,2,1,0:T(8,128)(2,1)}, u32[]{:S(2)}) copy-start(bf16[2,2,256,256]{3,2,1,0:T(8,128)(2,1)} %constant.19.clone.refs_8_.refs_9_) | copy-start | bytes 1572868
  19.0 1.0 %copy-start.4 = (bf16[2,3,256,128]{3,2,1,0:T(8,128)(2,1)S(1)}, bf16[2,3,256,128]{3,2,1,0:T(8,128)(2,1)}, u32[]{:S(2)}) copy-start(bf16[2,3,256,128]{3,2,1,0:T(8,128)(2,1)} %constant.20.clone.refs_9_.refs_10_) | copy-start | bytes 1179652
  20.0 0.9 %copy-start.5 = (bf16[1,48,2304]{2,1,0:T(8,128)(2,1)S(1)}, bf16[1,48,2304]{2,1,0:T(8,128)(2,1)}, u32[]{:S(2)}) copy-start(bf16[1,48,2304]{2,1,0:T(8,128)(2,1)} %refs_3_.3) | copy-start | bytes 663556
  20.9 0.7 %copy-start.6 = (bf16[48,144]{1,0:T(8,128)(2,1)S(1)}, bf16[48,144]{1,0:T(8,128)(2,1)}, u32[]{:S(2)}) copy-start(bf16[48,144]{1,0:T(8,128)(2,1)} %constant.18.clone.refs_7_.refs_8_) | copy-start | bytes 41476
  21.7 0.7 %copy-start.7 = (bf16[48,144]{1,0:T(8,128)(2,1)S(1)}, bf16[48,144]{1,0:T(8,128)(2,1)}, u32[]{:S(2)}) copy-start(bf16[48,144]{1,0:T(8,128)(2,1)} %constant.17.clone.refs_6_.refs_7_) | copy-start | bytes 41476
  22.4 0.7 %copy-start.8 = (bf16[48,144]{1,0:T(8,128)(2,1)S(1)}, bf16[48,144]{1,0:T(8,128)(2,1)}, u32[]{:S(2)}) copy-start(bf16[48,144]{1,0:T(8,128)(2,1)} %constant.16.clone.refs_5_.refs_6_) | copy-start | bytes 41476
  23.2 0.7 %copy-start.9 = (s32[3,2,512]{2,1,0:T(2,128)S(1)}, s32[3,2,512]{2,1,0:T(2,128)}, u32[]{:S(2)}) copy-start(s32[3,2,512]{2,1,0:T(2,128)} %refs_2_.3) | copy-start | bytes 36868
  23.9 13.8 %copy-start.1 = (f32[48,3072]{1,0:T(8,128)S(1)}, f32[48,3072]{1,0:T(8,128)}, u32[]{:S(2)}) copy-start(f32[48,3072]{1,0:T(8,128)} %constant.21.clone.refs_10_.refs_11_) | copy-start | bytes 1769476
  23.9 13.8 %copy-start.3 = (bf16[2,2,256,256]{3,2,1,0:T(8,128)(2,1)S(1)}, bf16[2,2,256,256]{3,2,1,0:T(8,128)(2,1)}, u32[]{:S(2)}) copy-start(bf16[2,2,256,256]{3,2,1,0:T(8,128)(2,1)} %constant.19.clone.refs_8_.refs_9_) | copy-start | bytes 1572868
